TPU v7x, 32 devices: a whole 2x2x4 slice. The times are simulated.
32 devices in a mesh: gx: 8 (over z, core), gy: 4 (over y, x).
Axes of the slice: x: 2, y: 2, z: 4, core: 2. Of those that a mesh axis runs over, the one named last changes fastest.
Arguments:
- density: float32 [512, 512, 512], P('gx', 'gy'), may hold values from -6 to 6
- radius_cells: int32 [2], replicated, may hold values from 1 to 32
Outputs:
- filtered: float32 [2, 512, 512, 512], P(None, 'gx', 'gy')
All inputs are finite; a program needn't handle non-finite values.
Results may differ from a plain program's by a relative error of at most 0.0001.
Values sent between devices are 32-bit elements; how exact they have to be, the bound alone decides.
A program may use at most 192 MiB of HBM per device.

v0:
```python
import math

import jax
import jax.numpy as jnp
from jax import lax
from jax.sharding import PartitionSpec as P

HIGHEST = lax.Precision.HIGHEST


def window(u_value):
    is_small = u_value < 0.2
    safe_u = jnp.where(is_small, 1.0, u_value)
    closed_form = 3.0 * (jnp.sin(safe_u) - safe_u * jnp.cos(safe_u)) / (safe_u * safe_u * safe_u)
    series = 1.0 - u_value * u_value / 10.0 + u_value**4 / 280.0
    return jnp.where(is_small, series, closed_form)


def dft_tables(length, direction):
    indices = jnp.arange(length, dtype=jnp.int32)
    product = indices[:, None] * indices[None, :] % length
    angles = 2.0 * math.pi / length * product.astype(jnp.float32)
    return (jnp.cos(angles), direction * jnp.sin(angles))


def twiddle_table(length, quarter, direction):
    row_ids = jnp.arange(4, dtype=jnp.int32)[:, None]
    col_ids = jnp.arange(quarter, dtype=jnp.int32)[None, :]
    angles = 2.0 * math.pi / length * (row_ids * col_ids % length).astype(jnp.float32)
    return (jnp.cos(angles), direction * jnp.sin(angles))


def product_section(real_part, imag_part, joined_form, cos_table, sin_table):
    block_table = jnp.stack(
        [jnp.stack([cos_table, sin_table], 1), jnp.stack([-sin_table, cos_table], 1)], 0
    )
    stacked = jnp.stack([real_part, imag_part], 0)
    result = jnp.einsum(
        joined_form, stacked, block_table, precision=HIGHEST, preferred_element_type=jnp.float32
    )
    return (result[0], result[1])


def rotate(real_part, imag_part, cos_table, sin_table):
    return (
        real_part * cos_table - imag_part * sin_table,
        real_part * sin_table + imag_part * cos_table,
    )


def radix_four(real_part, imag_part, along_axis, direction):
    reals = [lax.index_in_dim(real_part, offset, along_axis, keepdims=False) for offset in range(4)]
    imags = [lax.index_in_dim(imag_part, offset, along_axis, keepdims=False) for offset in range(4)]
    sum_even_re = reals[0] + reals[2]
    sum_even_im = imags[0] + imags[2]
    diff_even_re = reals[0] - reals[2]
    diff_even_im = imags[0] - imags[2]
    sum_odd_re = reals[1] + reals[3]
    sum_odd_im = imags[1] + imags[3]
    diff_odd_re = reals[1] - reals[3]
    diff_odd_im = imags[1] - imags[3]
    out_re = [
        sum_even_re + sum_odd_re,
        diff_even_re - direction * diff_odd_im,
        sum_even_re - sum_odd_re,
        diff_even_re + direction * diff_odd_im,
    ]
    out_im = [
        sum_even_im + sum_odd_im,
        diff_even_im + direction * diff_odd_re,
        sum_even_im - sum_odd_im,
        diff_even_im - direction * diff_odd_re,
    ]
    return (jnp.stack(out_re, along_axis), jnp.stack(out_im, along_axis))


def signed_squares(values, length):
    signed = jnp.where(values > length // 2, values - length, values).astype(jnp.float32)
    return signed * signed


def per_device(density, radius_cells):
    rows_x, rows_y, length = density.shape
    quarter = length // 4
    count_gx = lax.axis_size("gx")
    count_gy = lax.axis_size("gy")
    devices = count_gx * count_gy
    slab_rows = rows_x // count_gy
    band_rows = length // devices
    fwd_cos, fwd_sin = dft_tables(quarter, -1.0)
    inv_cos, inv_sin = dft_tables(quarter, 1.0)
    twid_fwd_cos, twid_fwd_sin = twiddle_table(length, quarter, -1.0)
    twid_inv_cos, twid_inv_sin = twiddle_table(length, quarter, 1.0)
    scale_factor = 1.0 / float(length) ** 3
    real_part = density.reshape(rows_x, rows_y, 4, quarter)
    imag_part = jnp.zeros_like(real_part)
    real_part, imag_part = radix_four(real_part, imag_part, 2, -1.0)
    real_part, imag_part = rotate(real_part, imag_part, twid_fwd_cos, twid_fwd_sin)
    real_part, imag_part = product_section(
        real_part, imag_part, "pxyab,pbqc->qxyac", fwd_cos, fwd_sin
    )
    part_re = lax.all_to_all(real_part, "gy", split_axis=0, concat_axis=1, tiled=True)
    part_im = lax.all_to_all(imag_part, "gy", split_axis=0, concat_axis=1, tiled=True)
    piece_rows = part_re.shape[0]
    slices = part_re.shape[2]
    shaped = (piece_rows, 4, quarter, slices, quarter)
    part_re = part_re.reshape(shaped)
    part_im = part_im.reshape(shaped)
    part_re, part_im = radix_four(part_re, part_im, 1, -1.0)
    part_re, part_im = rotate(
        part_re, part_im, twid_fwd_cos[None, :, :, None, None], twid_fwd_sin[None, :, :, None, None]
    )
    part_re, part_im = product_section(part_re, part_im, "piabcd,pbqe->qiaecd", fwd_cos, fwd_sin)
    flat_shape = (piece_rows, length, slices, quarter)
    real_part = part_re.reshape(flat_shape)
    imag_part = part_im.reshape(flat_shape)
    real_part = real_part.reshape(slab_rows, length, length)
    imag_part = imag_part.reshape(slab_rows, length, length)
    trail = real_part.shape[-1]
    moved_re, moved_im = (
        lax.all_to_all(real_part[None], ("gx", "gy"), split_axis=2, concat_axis=0, tiled=True),
        lax.all_to_all(imag_part[None], ("gx", "gy"), split_axis=2, concat_axis=0, tiled=True),
    )
    x_shape = (4, quarter, band_rows, trail)
    real_part = moved_re.reshape(x_shape)
    imag_part = moved_im.reshape(x_shape)
    real_part, imag_part = radix_four(real_part, imag_part, 0, -1.0)
    real_part, imag_part = rotate(
        real_part, imag_part, twid_fwd_cos[:, :, None, None], twid_fwd_sin[:, :, None, None]
    )
    real_part, imag_part = product_section(
        real_part, imag_part, "pabcd,pbqe->qaecd", fwd_cos, fwd_sin
    )
    pair_freq = (
        jnp.arange(4, dtype=jnp.int32)[:, None] + 4 * jnp.arange(quarter, dtype=jnp.int32)[None, :]
    )
    pair_squares = signed_squares(pair_freq, length)
    flat_band = lax.axis_index(("gx", "gy")) * band_rows + jnp.arange(band_rows, dtype=jnp.int32)
    band_freq = flat_band // quarter + 4 * (flat_band % quarter)
    band_squares = signed_squares(band_freq, length)
    trail_ids = jnp.arange(trail, dtype=jnp.int32)
    trail_freq = trail_ids // quarter + 4 * (trail_ids % quarter)
    trail_squares = signed_squares(trail_freq, length)
    k_squared = (
        pair_squares[:, :, None, None]
        + band_squares[None, None, :, None]
        + trail_squares[None, None, None, :]
    )
    k_length = 2.0 * math.pi / length * jnp.sqrt(k_squared)
    radius_values = radius_cells.astype(jnp.float32)
    weight_first = window(k_length * radius_values[0])
    weight_second = window(k_length * radius_values[1])
    packed_re = real_part * weight_first - imag_part * weight_second
    packed_im = imag_part * weight_first + real_part * weight_second
    rest = packed_re.shape[-1]
    packed_re, packed_im = product_section(
        packed_re, packed_im, "pabcd,pbqe->qaecd", inv_cos, inv_sin
    )
    packed_re, packed_im = rotate(
        packed_re, packed_im, twid_inv_cos[:, :, None, None], twid_inv_sin[:, :, None, None]
    )
    packed_re, packed_im = radix_four(packed_re, packed_im, 0, 1.0)
    flat_x = (length, band_rows, rest)
    back_re, back_im = (
        lax.all_to_all(
            packed_re.reshape(flat_x), ("gx", "gy"), split_axis=0, concat_axis=1, tiled=True
        ),
        lax.all_to_all(
            packed_im.reshape(flat_x), ("gx", "gy"), split_axis=0, concat_axis=1, tiled=True
        ),
    )
    y_shape = (slab_rows, 4, quarter, rest)
    packed_re = back_re.reshape(y_shape)
    packed_im = back_im.reshape(y_shape)
    packed_re, packed_im = product_section(
        packed_re, packed_im, "piabr,pbqe->qiaer", inv_cos, inv_sin
    )
    packed_re, packed_im = rotate(
        packed_re, packed_im, twid_inv_cos[None, :, :, None], twid_inv_sin[None, :, :, None]
    )
    packed_re, packed_im = radix_four(packed_re, packed_im, 1, 1.0)
    flat_y = (slab_rows, length, rest)
    packed_re, packed_im = (
        lax.all_to_all(packed_re.reshape(flat_y), "gy", split_axis=1, concat_axis=0, tiled=True),
        lax.all_to_all(packed_im.reshape(flat_y), "gy", split_axis=1, concat_axis=0, tiled=True),
    )
    z_shape = (rows_x, rows_y, 4, quarter)
    packed_re = packed_re.reshape(z_shape)
    packed_im = packed_im.reshape(z_shape)
    packed_re, packed_im = product_section(
        packed_re, packed_im, "pxyab,pbqc->qxyac", inv_cos, inv_sin
    )
    packed_re, packed_im = rotate(packed_re, packed_im, twid_inv_cos, twid_inv_sin)
    packed_re, packed_im = radix_four(packed_re, packed_im, 2, 1.0)
    field_first = packed_re.reshape(rows_x, rows_y, length) * scale_factor
    field_second = packed_im.reshape(rows_x, rows_y, length) * scale_factor
    return jnp.stack([field_first, field_second])


def solution(mesh):
    return jax.shard_map(
        per_device,
        mesh=mesh,
        in_specs=(P("gx", "gy", None), P()),
        out_specs=P(None, "gx", "gy", None),
        check_vma=False,
    )
```

profile of v0, /device:TPU:0, one launch (start us, length us, event | category | flops | bytes accessed | tf_op | source)
XLA Modules:
  0.0 3307.3 jit_solution(12067248718974111273)
XLA Ops:
  0.9 17.4 copy.102
  18.3 12.4 fusion.115
  53.2 11.8 add_bitcast_fusion.4
  68.3 19.1 multiply_subtract_fusion.6
  87.4 36.8 %fusion.22 = f32[2,64,128,4,128]{2,4,3,1,0:T(8,128)} fusion(f32[1,64,128,4,128]{4,2,0,3,1:T(8,128)} %get-tuple-element.42, f32[1,64,128,4,128]{4,2,0,3,1:T(8,128)S(1)} %get-tuple-element.41, f32[1,128,2,128]{1,3,0,2:T(8,128)S(1)} %get-tuple-element.73, f32[1,128,2,128]{1,3,0,2:T(8,128)S(1)} %get-tuple-element.74), kind=kOutput, calls=%fused_computation.37 | convolution fusion | flops 25778257920 | bytes 67371008 | tf_op jit(solution)/shard_map/pxyab,pbqc->qxyac/dot_general | solution.py:38
  124.2 17.7 slice_bitcast_fusion.7
  141.9 188.6 %all_to_all.120 = f32[64,128,4,128]{1,3,2,0:T(8,128)} all-to-all(f32[64,128,4,128]{1,3,2,0:T(8,128)S(1)} %get-tuple-element.39), channel_id=1, replica_groups=mesh['gx'=8,'gy'=4] {'gy'}, dimensions={0} | all-to-all | bytes 33554432 | tf_op jit(solution)/shard_map/all_to_all | solution.py:102
  330.5 7.5 all-to-all-start.1
  338.0 16.3 copy.111
  354.3 165.2 %all-to-all-done.1 = f32[64,128,4,128]{1,3,2,0:T(8,128)} async-done(((f32[64,128,4,128]{1,3,2,0:T(8,128)}), f32[64,128,4,128]{1,3,2,0:T(8,128)}, u32[]{:S(2)}, u32[]{:S(2)}) %all-to-all-start.1) | async-done | bytes 16777248 | tf_op jit(solution)/shard_map/all_to_all | solution.py:103
  519.6 16.3 copy.112
  535.9 9.5 add_bitcast_fusion.3
  545.4 17.8 subtract_bitcast_fusion.3
  563.1 9.5 add_bitcast_fusion.1
  572.6 16.4 multiply_subtract_fusion.5
  589.0 36.8 %fusion.21 = f32[2,16,4,128,4,128]{5,3,4,2,1,0:T(8,128)} fusion(f32[1,16,4,128,4,128]{5,3,0,4,2,1:T(8,128)} %get-tuple-element.16, f32[1,16,4,128,4,128]{5,3,0,4,2,1:T(8,128)S(1)} %get-tuple-element.15, f32[1,128,2,128]{1,3,0,2:T(8,128)S(1)} %get-tuple-element.73, f32[1,128,2,128]{1,3,0,2:T(8,128)S(1)} %get-tuple-element.74), kind=kOutput, calls=%fused_computation.36 | convolution fusion | flops 25778257920 | bytes 67371008 | tf_op jit(solution)/shard_map/piabcd,pbqe->qiaecd/dot_general | solution.py:38
  625.8 21.1 fusion.114
  646.9 19.1 copy.118
  666.0 18.6 copy.119
  689.5 19.0 copy.122
  708.5 18.7 copy.123
  727.2 345.0 %all-to-all-done.2 = f32[1,16,512,512]{3,0,1,2:T(1,128)} async-done(((f32[1,16,512,512]{3,0,1,2:T(1,128)}), f32[1,16,512,512]{3,0,1,2:T(1,128)}, u32[]{:S(2)}, u32[]{:S(2)}) %all-to-all-start.2) | async-done | bytes 16777248 | tf_op jit(solution)/shard_map/all_to_all | solution.py:121
  1078.1 11.0 copy.120
  1099.6 359.0 %all-to-all-done.3 = f32[1,16,512,512]{3,0,1,2:T(1,128)} async-done(((f32[1,16,512,512]{3,0,1,2:T(1,128)}), f32[1,16,512,512]{3,0,1,2:T(1,128)}, u32[]{:S(2)}, u32[]{:S(2)}) %all-to-all-start.3) | async-done | bytes 16777248 | tf_op jit(solution)/shard_map/all_to_all | solution.py:122
  1458.6 15.9 copy.124
  1474.5 17.9 fusion.38
  1492.4 7.5 fusion.40
  1525.8 16.1 multiply_subtract_fusion.4
  1542.0 39.4 %fusion.20 = f32[2,4,128,16,512]{4,2,3,1,0:T(8,128)S(1)} fusion(f32[1,4,128,16,512]{4,2,0,3,1:T(8,128)} %get-tuple-element.14, f32[1,4,128,16,512]{4,2,0,3,1:T(8,128)} %get-tuple-element.13, f32[1,128,2,128]{1,3,0,2:T(8,128)S(1)} %copy-done.20, f32[1,128,2,128]{1,3,0,2:T(8,128)S(1)} %copy-done.22), kind=kOutput, calls=%fused_computation.35 | convolution fusion | flops 25778257920 | bytes 67371008 | tf_op jit(solution)/shard_map/pabcd,pbqe->qaecd/dot_general | solution.py:38
  1581.4 145.4 %multiply_subtract_fusion.3 = (f32[1,4,128,16,512]{4,2,3,1,0:T(8,128)}, f32[1,4,128,16,512]{4,2,3,1,0:T(8,128)}) fusion(f32[2,4,128,16,512]{4,2,3,1,0:T(8,128)S(1)} %fusion.20, f32[]{:T(128)} %bitcast.68, f32[512]{0:T(512)S(1)} %fusion.98, f32[4,128,16]{1,2,0:T(8,128)S(1)} %broadcast_add_fusion, f32[]{:T(128)} %bitcast.70), kind=kLoop, calls=%fused_computation.74 | loop fusion | flops 163577856 | bytes 67143688 | tf_op jit(solution)/shard_map/sub | solution.py:153
  1726.8 37.0 %fusion.23 = f32[2,4,128,16,512]{4,2,3,1,0:T(8,128)} fusion(f32[1,4,128,16,512]{4,2,3,1,0:T(8,128)} %get-tuple-element.6, f32[1,4,128,16,512]{4,2,3,1,0:T(8,128)} %get-tuple-element.5, f32[1,128,2,128]{1,3,2,0:T(8,128)S(1)} %copy-done.18, f32[1,128,2,128]{1,3,2,0:T(8,128)S(1)} %copy-done.17), kind=kOutput, calls=%fused_computation.38 | convolution fusion | flops 25778257920 | bytes 67371008 | tf_op jit(solution)/shard_map/pabcd,pbqe->qaecd/dot_general | solution.py:38
  1763.9 16.9 multiply_add_fusion.2
  1791.3 17.4 fusion.46
  1814.9 11.7 copy.134
  1830.7 7.3 fusion.50
  1841.4 11.8 copy.136
  1853.2 359.9 %all-to-all-done.4 = f32[512,16,512]{2,1,0:T(8,128)} async-done(((f32[512,16,512]{2,1,0:T(8,128)}), f32[512,16,512]{2,1,0:T(8,128)}, u32[]{:S(2)}, u32[]{:S(2)}) %all-to-all-start.4) | async-done | bytes 16777248 | tf_op jit(solution)/shard_map/all_to_all | solution.py:165
  2217.1 12.3 copy.135
  2229.4 370.2 %all-to-all-done.5 = f32[512,16,512]{2,1,0:T(8,128)} async-done(((f32[512,16,512]{2,1,0:T(8,128)}), f32[512,16,512]{2,1,0:T(8,128)}, u32[]{:S(2)}, u32[]{:S(2)}) %all-to-all-start.5) | async-done | bytes 16777248 | tf_op jit(solution)/shard_map/all_to_all | solution.py:168
  2599.6 7.0 copy.137
  2610.2 37.8 %fusion.19 = f32[2,16,4,128,512]{4,3,2,1,0:T(8,128)} fusion(f32[1,16,4,128,512]{4,3,0,2,1:T(8,128)S(1)} %bitcast.282, f32[1,16,4,128,512]{4,3,0,2,1:T(8,128)S(1)} %bitcast.281, f32[1,128,2,128]{1,3,2,0:T(8,128)S(1)} %copy-done.18, f32[1,128,2,128]{1,3,2,0:T(8,128)S(1)} %copy-done.17), kind=kOutput, calls=%fused_computation.34 | convolution fusion | flops 25778257920 | bytes 67371008 | tf_op jit(solution)/shard_map/piabr,pbqe->qiaer/dot_general | solution.py:38
  2648.0 17.0 multiply_add_fusion.1
  2675.5 17.4 fusion.54
  2692.9 6.2 pad_maximum_fusion.10
  2699.1 21.4 copy.139
  2720.5 7.0 all-to-all-start.6
  2727.6 7.4 fusion.58
  2738.3 21.0 copy.142
  2759.3 150.4 %all-to-all-done.6 = f32[16,512,512]{2,0,1:T(8,128)} async-done(((f32[16,512,512]{2,0,1:T(8,128)}), f32[16,512,512]{2,0,1:T(8,128)}, u32[]{:S(2)}, u32[]{:S(2)}) %all-to-all-start.6) | async-done | bytes 16777248 | tf_op jit(solution)/shard_map/all_to_all | solution.py:184
  2909.7 7.2 all-to-all-start.7
  2916.9 19.5 copy.141
  2936.4 17.5 copy.145
  2953.9 144.8 %all-to-all-done.7 = f32[16,512,512]{2,0,1:T(8,128)} async-done(((f32[16,512,512]{2,0,1:T(8,128)}), f32[16,512,512]{2,0,1:T(8,128)}, u32[]{:S(2)}, u32[]{:S(2)}) %all-to-all-start.7) | async-done | bytes 16777248 | tf_op jit(solution)/shard_map/all_to_all | solution.py:185
  3098.7 19.4 copy.144
  3118.1 17.4 copy.146
  3135.5 36.8 %fusion.18 = f32[2,64,128,4,128]{2,4,3,1,0:T(8,128)} fusion(f32[1,64,128,4,128]{4,2,0,3,1:T(8,128)} %copy.146, f32[1,64,128,4,128]{4,2,0,3,1:T(8,128)} %copy.145, f32[1,128,2,128]{1,3,2,0:T(8,128)S(1)} %copy-done.18, f32[1,128,2,128]{1,3,2,0:T(8,128)S(1)} %copy-done.17), kind=kOutput, calls=%fused_computation.33 | convolution fusion | flops 25778257920 | bytes 67371008 | tf_op jit(solution)/shard_map/pxyab,pbqc->qxyac/dot_general | solution.py:38
  3172.4 17.2 multiply_add_fusion
  3199.9 17.9 fusion.62
  3217.8 9.8 fusion.66
  3230.3 6.3 maximum_multiply_fusion
  3236.6 17.4 copy.148
  3254.0 12.0 maximum_multiply_fusion.1
  3266.0 17.5 copy.149
  3283.5 23.7 pad_maximum_fusion.1
  (93 shorter events, 131.0 us)
Async XLA Ops:
  0.1 572.6 %copy-start.23 = (f32[4,128]{1,0:T(4,128)}, f32[4,128]{1,0:T(4,128)S(1)}, u32[]{:S(2)}) copy-start(f32[4,128]{1,0:T(4,128)S(1)} %get-tuple-element.79) | copy-start | bytes 6148
  0.1 572.6 %copy-start.25 = (f32[4,128]{1,0:T(4,128)}, f32[4,128]{1,0:T(4,128)S(1)}, u32[]{:S(2)}) copy-start(f32[4,128]{1,0:T(4,128)S(1)} %get-tuple-element.78) | copy-start | bytes 6148
  65.7 523.3 %copy-start.19 = (f32[1,128,2,128]{1,3,0,2:T(8,128)}, f32[1,128,2,128]{1,3,0,2:T(8,128)S(1)}, u32[]{:S(2)}) copy-start(f32[1,128,2,128]{1,3,0,2:T(8,128)S(1)} %get-tuple-element.73) | copy-start | bytes 393220
  65.7 523.3 %copy-start.21 = (f32[1,128,2,128]{1,3,0,2:T(8,128)}, f32[1,128,2,128]{1,3,0,2:T(8,128)S(1)}, u32[]{:S(2)}) copy-start(f32[1,128,2,128]{1,3,0,2:T(8,128)S(1)} %get-tuple-element.74) | copy-start | bytes 393220
  330.5 189.1 %all-to-all-start.1 = ((f32[64,128,4,128]{1,3,2,0:T(8,128)}), f32[64,128,4,128]{1,3,2,0:T(8,128)}, u32[]{:S(2)}, u32[]{:S(2)}) async-start(f32[64,128,4,128]{1,3,2,0:T(8,128)} %get-tuple-element.40), calls=%async_computation.1 | async-start | bytes 33554432 | tf_op jit(solution)/shard_map/all_to_all | solution.py:103
  684.7 387.5 %all-to-all-start.2 = ((f32[1,16,512,512]{3,0,1,2:T(1,128)}), f32[1,16,512,512]{3,0,1,2:T(1,128)}, u32[]{:S(2)}, u32[]{:S(2)}) async-start(f32[1,16,512,512]{3,0,1,2:T(1,128)} %copy.119), calls=%async_computation.2 | async-start | bytes 33554432 | tf_op jit(solution)/shard_map/all_to_all | solution.py:121
  727.2 348.9 %copy-start.27 = (s32[2]{0:T(128)S(1)}, s32[2]{0:T(128)}, u32[]{:S(2)}) copy-start(s32[2]{0:T(128)} %param.3) | copy-start | bytes 28
  1072.2 386.4 %all-to-all-start.3 = ((f32[1,16,512,512]{3,0,1,2:T(1,128)}), f32[1,16,512,512]{3,0,1,2:T(1,128)}, u32[]{:S(2)}, u32[]{:S(2)}) async-start(f32[1,16,512,512]{3,0,1,2:T(1,128)} %copy.123), calls=%async_computation.3 | async-start | bytes 33554432 | tf_op jit(solution)/shard_map/all_to_all | solution.py:122
  1089.1 6.2 copy-start
  1492.4 7.6 copy-start.7
  1492.4 10.0 copy-start.6
  1492.4 12.5 copy-start.5
  1500.0 9.8 copy-start.9
  1502.5 10.0 copy-start.8
  1509.8 16.0 copy-start.24
  1509.8 16.0 copy-start.26
  1525.8 16.1 copy-start.20
  1525.8 16.1 copy-start.22
  1581.4 145.5 %copy-start.17 = (f32[1,128,2,128]{1,3,2,0:T(8,128)S(1)}, f32[1,128,2,128]{1,3,2,0:T(8,128)}, u32[]{:S(2)}) copy-start(f32[1,128,2,128]{1,3,2,0:T(8,128)} %get-tuple-element.72) | copy-start | bytes 393220
  1581.4 145.5 %copy-start.18 = (f32[1,128,2,128]{1,3,2,0:T(8,128)S(1)}, f32[1,128,2,128]{1,3,2,0:T(8,128)}, u32[]{:S(2)}) copy-start(f32[1,128,2,128]{1,3,2,0:T(8,128)} %get-tuple-element.75) | copy-start | bytes 393220
  1780.8 6.2 copy-start.2
  1826.6 386.6 %all-to-all-start.4 = ((f32[512,16,512]{2,1,0:T(8,128)}), f32[512,16,512]{2,1,0:T(8,128)}, u32[]{:S(2)}, u32[]{:S(2)}) async-start(f32[512,16,512]{2,1,0:T(8,128)} %bitcast.269), calls=%async_computation.4 | async-start | bytes 33554432 | tf_op jit(solution)/shard_map/all_to_all | solution.py:165
  1830.7 7.4 copy-start.10
  1830.7 8.3 copy-start.11
  2213.2 386.4 %all-to-all-start.5 = ((f32[512,16,512]{2,1,0:T(8,128)}), f32[512,16,512]{2,1,0:T(8,128)}, u32[]{:S(2)}, u32[]{:S(2)}) async-start(f32[512,16,512]{2,1,0:T(8,128)} %bitcast.270), calls=%async_computation.5 | async-start | bytes 33554432 | tf_op jit(solution)/shard_map/all_to_all | solution.py:168
  2599.6 10.6 copy-start.4
  2665.0 6.2 copy-start.3
  2720.5 189.2 %all-to-all-start.6 = ((f32[16,512,512]{2,0,1:T(8,128)}), f32[16,512,512]{2,0,1:T(8,128)}, u32[]{:S(2)}, u32[]{:S(2)}) async-start(f32[16,512,512]{2,0,1:T(8,128)} %copy.139), calls=%async_computation.6 | async-start | bytes 33554432 | tf_op jit(solution)/shard_map/all_to_all | solution.py:184
  2727.5 7.4 copy-start.12
  2727.6 8.3 copy-start.13
  2909.7 188.9 %all-to-all-start.7 = ((f32[16,512,512]{2,0,1:T(8,128)}), f32[16,512,512]{2,0,1:T(8,128)}, u32[]{:S(2)}, u32[]{:S(2)}) async-start(f32[16,512,512]{2,0,1:T(8,128)} %copy.142), calls=%async_computation.7 | async-start | bytes 33554432 | tf_op jit(solution)/shard_map/all_to_all | solution.py:185
  3189.6 6.2 copy-start.1
  3217.8 9.8 copy-start.14
  3217.8 11.4 copy-start.15
  3217.8 12.5 copy-start.16
where the time goes:
time: 3320 us; the launch traced here: 3310 us
  waiting for transfers between devices  1890 us (57%)
  local copies, waits for them, and re-layouts  482 us (15%)
  other arithmetic  477 us (14%)
  matrix products  225 us (7%)
  blocking collectives  189 us (6%)
  starting transfers between devices  38.4 us (1%)
    all_to_all x1, waiting for transfers between devices, per_device(): lax.all_to_all(packed_im.reshape(flat_x), ('gx', 'gy'), split_axis=0, con...  370 us
    all_to_all x1, waiting for transfers between devices, per_device(): lax.all_to_all(packed_re.reshape(flat_x), ('gx', 'gy'), split_axis=0, con...  360 us
    all_to_all x1, waiting for transfers between devices, per_device(): lax.all_to_all(imag_part[None], ('gx', 'gy'), split_axis=2, concat_axis=0...  359 us
    all_to_all x1, waiting for transfers between devices, per_device(): lax.all_to_all(real_part[None], ('gx', 'gy'), split_axis=2, concat_axis=0...  345 us
    dot_general x6, matrix products, product_section(): jnp.einsum(joined_form, stacked, block_table, precision=HIGHEST, preferre...  225 us
    all_to_all x1, blocking collectives, per_device(): lax.all_to_all(real_part, 'gy', split_axis=0, concat_axis=1, tiled=True)  189 us
    all_to_all x1, waiting for transfers between devices, per_device(): lax.all_to_all(imag_part, 'gy', split_axis=0, concat_axis=1, tiled=True)  165 us
    all_to_all x1, waiting for transfers between devices, per_device(): lax.all_to_all(packed_re.reshape(flat_y), 'gy', split_axis=1, concat_axis...  150 us
  transfers between devices with their start and end apart: 7, of which 7 were waited for; matrix products, arithmetic and copies ran while one was open for 5% of the time, Pallas kernels for 0%

commit v1 on v0

v1 whole, which is shorter than its diff:
```python
import math

import jax
import jax.numpy as jnp
import numpy as np
from jax import lax
from jax.sharding import PartitionSpec as P

PREC = lax.Precision.HIGH


def window(k_squared, scale_squared):
    u_squared = k_squared * scale_squared
    u_value = jnp.sqrt(u_squared)
    is_small = u_value < 0.2
    safe = jnp.where(is_small, 1.0, u_value)
    turns = jnp.floor(safe * (1.0 / math.pi) + 0.5)
    rest = safe - turns * 3.140625
    rest = rest - turns * 9.67502593994140625e-4
    rest = rest - turns * 1.509957990978376432e-7
    s2 = rest * rest
    sin_v = rest * (1.0 + s2 * (-1.6666666666e-1 + s2 * (8.3333333e-3 + s2 * (
        -1.98412698e-4 + s2 * (2.75573192e-6 + s2 * -2.50521084e-8)))))
    cos_v = 1.0 + s2 * (-0.5 + s2 * (4.16666666e-2 + s2 * (-1.38888889e-3 + s2 * (
        2.48015873e-5 + s2 * (-2.75573192e-7 + s2 * 2.08767570e-9)))))
    half = turns * 0.5
    sign = jnp.where(half == jnp.floor(half), 3.0, -3.0)
    closed = sign * (sin_v - safe * cos_v) / (safe * safe * safe)
    series = 1.0 - u_squared / 10.0 + u_squared * u_squared / 280.0
    return jnp.where(is_small, series, closed)


def times_i(values, half):
    return jnp.concatenate([-values[..., half:], values[..., :half]], -1)


def doubled(values, half):
    return jnp.concatenate([values, times_i(values, half)], 0)


def squares(values, length):
    signed = jnp.where(values > length // 2, values - length, values).astype(jnp.float32)
    return signed * signed


def dot(spec, left, right):
    return jnp.einsum(spec, left, right, precision=PREC, preferred_element_type=jnp.float32)


def trig(rows, cols, length):
    angles = 2.0 * math.pi / length * (np.outer(rows, cols) % length)
    return np.cos(angles), np.sin(angles)


def y_order(length, parts):
    half = length // parts // 2
    base = np.arange(length // 2).reshape(parts, half)
    mirror = (length - base) % length
    mirror[0, 0] = length // 2
    return np.concatenate([base, mirror], 1).reshape(-1)


def per_device(density, radius_cells):
    rows_x, rows_y, length = density.shape
    count_gx = lax.axis_size("gx")
    count_gy = lax.axis_size("gy")
    mid = length // 2
    half = mid // count_gy
    lanes = 2 * half
    cols_y = length // count_gx
    f32 = jnp.float32
    cells = np.arange(length)
    order = y_order(length, count_gx)

    cos_z, sin_z = trig(cells, np.arange(mid), length)
    fwd_im = -sin_z
    fwd_im[:, 0] = np.where(cells % 2 == 0, 1.0, -1.0)
    fwd_z = np.stack([cos_z, fwd_im], 1).reshape(length, 2, count_gy, half)
    fwd_z = jnp.asarray(fwd_z.transpose(2, 0, 1, 3).reshape(count_gy, length, lanes), f32)
    gain = np.full((mid,), 2.0 / float(length) ** 3)
    gain[0] = 1.0 / float(length) ** 3
    inv_re = cos_z * gain
    inv_im = -sin_z * gain
    inv_im[:, 0] = np.where(cells % 2 == 0, 1.0, -1.0) * gain[0]
    inv_z = np.stack([inv_re, inv_im], 1).reshape(length, 2, count_gy, half)
    inv_z = jnp.asarray(inv_z.transpose(2, 1, 3, 0).reshape(length, length), f32)
    cos_y, sin_y = trig(order, cells, length)
    fwd_y = jnp.asarray(np.concatenate([cos_y, sin_y], 1), f32)
    fwd_y = fwd_y * jnp.where(jnp.arange(2 * length) < length, 1.0, -1.0)
    inv_y = jnp.asarray(np.concatenate([cos_y.T, sin_y.T], 1), f32)
    cos_x, sin_x = trig(cells, cells, length)
    inv_x = jnp.asarray(np.concatenate([cos_x, sin_x], 1), f32)
    fwd_x = inv_x * jnp.where(jnp.arange(2 * length) < length, 1.0, -1.0)

    values = dot("xyz,bzl->byxl", density, fwd_z)
    values = lax.all_to_all(values, "gy", split_axis=0, concat_axis=0, tiled=True)
    values = values.reshape(length, rows_x, lanes)
    values = dot("qy,yxl->qxl", fwd_y, doubled(values, half))
    values = values.reshape(count_gx, cols_y, rows_x, lanes).transpose(0, 2, 1, 3)
    values = lax.all_to_all(values, "gx", split_axis=0, concat_axis=0, tiled=True)
    values = values.reshape(length, cols_y, lanes)
    values = dot("kx,xql->kql", fwd_x, doubled(values, half))

    part_x = lax.axis_index("gx")
    part_y = lax.axis_index("gy")
    kx_sq = squares(jnp.arange(length, dtype=jnp.int32), length)
    local = jnp.arange(cols_y, dtype=jnp.int32)
    base = part_x * (cols_y // 2) + local % (cols_y // 2)
    ky = jnp.where(local < cols_y // 2, base, (length - base) % length)
    ky = jnp.where((part_x == 0) & (local == cols_y // 2), mid, ky)
    ky_sq = squares(ky, length)
    lane = jnp.arange(lanes, dtype=jnp.int32)
    kz_sq = squares(part_y * half + lane % half, length)
    plane_sq = kx_sq[:, None] + ky_sq[None, :]
    cube_sq = plane_sq[:, :, None] + kz_sq[None, None, :]

    own_re = values[:, :, 0]
    own_im = values[:, :, half]

    def mirror(plane):
        plane = jnp.roll(jnp.flip(plane, 0), 1, 0)
        swapped = jnp.roll(plane, cols_y // 2, 1)
        itself = (part_x == 0) & (local % (cols_y // 2) == 0)
        return jnp.where(itself[None, :], plane, swapped)

    far_re, far_im = mirror(own_re), mirror(own_im)
    first = part_y == 0
    outs = []
    for index in range(radius_cells.shape[0]):
        scale = 2.0 * math.pi / length * radius_cells[index].astype(f32)
        scale = scale * scale
        weight = window(cube_sq, scale)
        low = window(plane_sq, scale)
        high = window(plane_sq + float(mid) ** 2, scale)
        mean, diff = 0.5 * (low + high), 0.5 * (low - high)
        fix_re = own_re * mean + far_re * diff
        fix_im = own_im * mean - far_im * diff
        field = values * weight
        field = jnp.where(first & (lane == 0), fix_re[:, :, None], field)
        field = jnp.where(first & (lane == half), fix_im[:, :, None], field)
        field = dot("xk,kql->xql", inv_x, doubled(field, half))
        field = field.reshape(count_gx, rows_x, cols_y, lanes)
        outs.append(lax.all_to_all(field, "gx", split_axis=0, concat_axis=0, tiled=True))
    results = []
    for field in outs:
        field = field.transpose(0, 2, 1, 3).reshape(length, rows_x, lanes)
        field = dot("yq,qxl->yxl", inv_y, doubled(field, half))
        field = field.reshape(count_gy, rows_y, rows_x, lanes)
        field = lax.all_to_all(field, "gy", split_axis=0, concat_axis=0, tiled=True)
        field = dot("gyxl,glz->xyz", field, inv_z.reshape(count_gy, lanes, length))
        results.append(field)
    return jnp.stack(results)


def solution(mesh):
    return jax.shard_map(
        per_device,
        mesh=mesh,
        in_specs=(P("gx", "gy", None), P()),
        out_specs=P(None, "gx", "gy", None),
        check_vma=False,
    )
```

time: 3320 us -> 2040 us (0.61)
  waiting for transfers between devices: 1890 us -> 1420 us
  local copies, waits for them, and re-layouts: 482 us -> 127 us
  other arithmetic: 477 us -> 188 us
  blocking collectives: 189 us -> 0 us
    all_to_all x7 -> x6, waiting for transfers between devices: 1890 us -> 1420 us  [the longest x2 605 us: per_device(): lax.all_to_all(field, 'gx', split_axis=0, concat_axis=0, tiled=True)]
    sub x8 -> x0, other arithmetic: 268 us -> none  [the longest x1 145 us: per_device(): packed_re = real_part * weight_first - imag_part * weight_second]
    all_to_all x1 -> x0, blocking collectives: 189 us -> none  [per_device(): lax.all_to_all(real_part, 'gy', split_axis=0, concat_axis=1, tiled=True)]
    all_to_all x8 -> x0, local copies, waits for them, and re-layouts: 118 us -> none  [the longest x1 19.5 us: per_device(): lax.all_to_all(packed_re.reshape(flat_y), 'gy', split_axis=1, concat_axis...]
    add x12 -> x1, other arithmetic: 100 us -> 0.08 us  [per_device(): plane_sq = kx_sq[:, None] + ky_sq[None, :]]
    another operation x7 -> x0, local copies, waits for them, and re-layouts: 98.3 us -> none  [the longest x2 34.9 us: product_section(): stacked = jnp.stack([real_part, imag_part], 0)]
    another operation x10 -> x1, other arithmetic: 90.3 us -> 11.4 us  [per_device(): return jnp.stack(results)]
    neg x1 -> x6, other arithmetic: 0.26 us -> 78 us  [times_i(): return jnp.concatenate([-values[..., half:], values[..., :half]], -1)]
  transfers between devices with their start and end apart: 7 -> 6, of which waited for: 7 -> 6; matrix products, arithmetic and copies ran while one was open for 5% -> 10% of each run, Pallas kernels for 0% -> 0%
where the time goes in v1:
time: 2040 us; the launch traced here: 2030 us
  waiting for transfers between devices  1420 us (70%)
  matrix products  257 us (13%)
  other arithmetic  188 us (9%)
  local copies, waits for them, and re-layouts  127 us (6%)
  starting transfers between devices  39.2 us (2%)
    all_to_all x2, waiting for transfers between devices, per_device(): lax.all_to_all(field, 'gx', split_axis=0, concat_axis=0, tiled=True)  605 us
    all_to_all x1, waiting for transfers between devices, per_device(): lax.all_to_all(values, 'gx', split_axis=0, concat_axis=0, tiled=True)  361 us
    all_to_all x2, waiting for transfers between devices, per_device(): field = lax.all_to_all(field, 'gy', split_axis=0, concat_axis=0, tiled=True)  271 us
    dot_general x8, matrix products, dot(): jnp.einsum(spec, left, right, precision=PREC, preferred_element_type=jnp....  226 us
    all_to_all x1, waiting for transfers between devices, per_device(): lax.all_to_all(values, 'gy', split_axis=0, concat_axis=0, tiled=True)  184 us
    neg x6, other arithmetic, times_i(): return jnp.concatenate([-values[..., half:], values[..., :half]], -1)  78 us
    select_n x1, other arithmetic, per_device(): field = jnp.where(first & (lane == half), fix_im[:, :, None], field)  72.5 us
  transfers between devices with their start and end apart: 6, of which 6 were waited for; matrix products, arithmetic and copies ran while one was open for 10% of the time, Pallas kernels for 0%

profile of v1, /device:TPU:0, one launch (start us, length us, event | category | flops | bytes accessed | tf_op | source)
XLA Modules:
  0.0 2034.6 jit_solution(5555310782021072428)
XLA Ops:
  0.0 18.9 fusion.84
  18.9 7.0 all-to-all-start
  25.9 183.8 %all-to-all-done = f32[4,128,64,128]{1,3,2,0:T(8,128)} async-done(((f32[4,128,64,128]{1,3,2,0:T(8,128)}), f32[4,128,64,128]{1,3,2,0:T(8,128)}, u32[]{:S(2)}, u32[]{:S(2)}) %all-to-all-start) | async-done | bytes 16777248 | tf_op jit(solution)/shard_map/all_to_all | solution.py:96
  209.7 17.5 copy.70
  227.2 23.7 %slice_negate_fusion.2 = (f32[512,64,64]{2,0,1:T(8,128)}, f32[512,64,64]{2,0,1:T(8,128)}) fusion(f32[512,64,128]{2,0,1:T(8,128)} %bitcast.94), kind=kLoop, calls=%fused_computation.80 | loop fusion | flops 2097152 | bytes 33554432 | tf_op jit(solution)/shard_map/neg | solution.py:34
  250.9 0.0 copy-done.9
  250.9 36.8 %fusion = f32[512,64,128]{2,0,1:T(8,128)} fusion(f32[512,64,64]{2,0,1:T(8,128)} %get-tuple-element.24, f32[512,64,64]{2,0,1:T(8,128)} %get-tuple-element.23, f32[512,64,128]{2,0,1:T(8,128)} %bitcast.95, f32[512,1024]{1,0:T(8,128)S(1)} %copy-done.9, f32[1024]{0:T(1024)S(1)} %fusion.199), kind=kOutput, calls=%fused_computation | convolution fusion | flops 25787105280 | bytes 52432896 | tf_op jit(solution)/shard_map/qy,yxl->qxl/dot_general | solution.py:47
  287.7 12.0 copy.86
  299.7 6.1 all-to-all-start.1
  305.8 0.0 copy-done.5
  305.8 0.6 fusion.216
  307.8 0.1 broadcast_add_fusion
  307.9 361.5 %all-to-all-done.1 = f32[8,64,64,128]{3,2,1,0:T(8,128)} async-done(((f32[8,64,64,128]{3,2,1,0:T(8,128)}), f32[8,64,64,128]{3,2,1,0:T(8,128)}, u32[]{:S(2)}, u32[]{:S(2)}) %all-to-all-start.1) | async-done | bytes 16777248 | tf_op jit(solution)/shard_map/all_to_all | solution.py:100
  669.4 17.6 copy.46
  687.0 11.1 slice_negate_fusion.5
  698.1 23.7 %maximum_maximum_fusion = f32[1024,64,128]{0,2,1:T(8,128)} fusion(f32[512,64,64]{0,2,1:T(8,128)} %get-tuple-element.22, f32[512,64,64]{0,2,1:T(8,128)} %get-tuple-element.21, f32[512,64,128]{0,2,1:T(8,128)} %copy.46), kind=kLoop, calls=%fused_computation.6 | loop fusion | flops 16777216 | bytes 67108864 | tf_op jit(solution)/shard_map/concatenate | solution.py:38
  721.8 0.0 copy-done.8
  721.8 30.4 %fusion.89 = f32[512,8192]{0,1:S(1)} fusion(f32[1024,8192]{0,1:T(8,128)} %bitcast.101, f32[512,1024]{1,0:T(8,128)S(1)} %copy-done.8, f32[1024]{0:T(1024)S(1)} %fusion.199), kind=kOutput, calls=%fused_computation.114 | convolution fusion | flops 25770328064 | bytes 52432896
  752.2 0.0 copy-start.3
  752.2 0.1 fusion.213
  752.3 6.1 copy-done.3
  758.3 0.6 fusion.214
  759.0 0.3 reverse.4
  759.3 0.1 slice_bitcast_fusion.1
  759.4 0.1 slice.174
  759.5 0.5 reverse.5
  760.1 0.1 slice_bitcast_fusion
  760.2 0.1 slice.175
  760.3 1.7 fusion.215
  762.0 0.1 fusion.194
  762.1 0.1 fusion.196
  762.2 1.2 add_bitcast_fusion.1
  763.4 1.2 subtract_bitcast_fusion.1
  764.5 72.5 %select_select_fusion.1 = (f32[512,64,128]{0,2,1:T(8,128)}, f32[512,64,128]{0,2,1:T(8,128)S(1)}) fusion(f32[512,64,128]{0,2,1:T(8,128)} %bitcast.105, f32[]{:T(128)} %bitcast.16, f32[128]{0:T(128)S(1)} %fusion.207, f32[512,64]{0,1:T(8,128)S(1)} %broadcast_add_fusion, f32[512,64]{0,1:T(8,128)S(1)} %get-tuple-element.27, f32[512,64]{0,1:T(8,128)S(1)} %get-tuple-element.25, ...), kind=kLoop, calls=%fused_computation.95 | loop fusion | flops 465567744 | bytes 50987784 | tf_op jit(solution)/shard_map/jit(_where)/select_n | solution.py:140
  837.1 7.3 slice_negate_fusion.3
  844.4 31.7 %fusion.18 = f32[512,64,128]{2,0,1:T(8,128)} fusion(f32[512,1024,1]{1,0,2:T(8,128)S(1)} %copy-done.7, f32[512,64,64]{0,2,1:T(8,128)} %get-tuple-element.14, f32[512,64,64]{0,2,1:T(8,128)} %get-tuple-element.13, f32[512,64,128]{0,2,1:T(8,128)S(1)} %get-tuple-element.6), kind=kOutput, calls=%fused_computation.19 | convolution fusion | flops 25786580992 | bytes 52428800 | tf_op jit(solution)/shard_map/xk,kql->xql/dot_general | solution.py:47
  876.1 11.8 copy.60
  887.9 5.7 all-to-all-start.4
  893.6 9.8 slice_negate_fusion.4
  903.4 30.0 %fusion.6 = f32[512,64,128]{2,0,1:T(8,128)S(1)} fusion(f32[512,1024,1]{1,0,2:T(8,128)S(1)} %copy-done.7, f32[512,64,64]{0,2,1:T(8,128)} %get-tuple-element.10, f32[512,64,64]{0,2,1:T(8,128)S(1)} %get-tuple-element.9, f32[512,64,128]{0,2,1:T(8,128)} %get-tuple-element.5), kind=kOutput, calls=%fused_computation.7 | convolution fusion | flops 25786580992 | bytes 52428800 | tf_op jit(solution)/shard_map/xk,kql->xql/dot_general | solution.py:47
  933.4 6.5 copy.55
  939.9 317.3 %all-to-all-done.4 = f32[8,64,64,128]{3,1,2,0:T(8,128)} async-done(((f32[8,64,64,128]{3,1,2,0:T(8,128)}), f32[8,64,64,128]{3,1,2,0:T(8,128)}, u32[]{:S(2)}, u32[]{:S(2)}) %all-to-all-start.4) | async-done | bytes 16777248 | tf_op jit(solution)/shard_map/all_to_all | solution.py:143
  1257.2 5.9 all-to-all-start.2
  1263.2 11.0 copy.61
  1274.2 0.0 copy-start.6
  1274.2 12.4 slice_negate_fusion
  1286.6 4.0 copy-done.1
  1290.6 0.0 copy-done.6
  1290.6 36.5 %fusion.24 = f32[512,64,128]{2,0,1:T(8,128)} fusion(f32[512,1024,1]{1,0,2:T(8,128)S(1)} %copy-done.6, f32[512,64,64]{2,0,1:T(8,128)} %get-tuple-element.12, f32[512,64,64]{2,0,1:T(8,128)} %get-tuple-element.11, f32[512,64,128]{2,0,1:T(8,128)} %bitcast.99), kind=kOutput, calls=%fused_computation.25 | convolution fusion | flops 25786580992 | bytes 52428800 | tf_op jit(solution)/shard_map/yq,qxl->yxl/dot_general | solution.py:47
  1327.1 11.8 copy.62
  1338.9 287.9 %all-to-all-done.2 = f32[8,64,64,128]{3,1,2,0:T(8,128)} async-done(((f32[8,64,64,128]{3,1,2,0:T(8,128)}), f32[8,64,64,128]{3,1,2,0:T(8,128)}, u32[]{:S(2)}, u32[]{:S(2)}) %all-to-all-start.2) | async-done | bytes 16777248 | tf_op jit(solution)/shard_map/all_to_all | solution.py:143
  1626.8 7.2 all-to-all-start.5
  1634.0 11.0 copy.56
  1645.0 13.7 slice_negate_fusion.1
  1658.8 2.1 copy-done
  1660.9 36.5 %fusion.12 = f32[512,64,128]{2,0,1:T(8,128)} fusion(f32[512,1024,1]{1,0,2:T(8,128)S(1)} %copy-done.6, f32[512,64,64]{2,0,1:T(8,128)} %get-tuple-element.8, f32[512,64,64]{2,0,1:T(8,128)} %get-tuple-element.7, f32[512,64,128]{2,0,1:T(8,128)} %bitcast.97), kind=kOutput, calls=%fused_computation.13 | convolution fusion | flops 25786580992 | bytes 52428800 | tf_op jit(solution)/shard_map/yq,qxl->yxl/dot_general | solution.py:47
  1697.4 11.7 copy.57
  1709.0 107.2 %all-to-all-done.5 = f32[4,128,64,128]{3,1,2,0:T(8,128)} async-done(((f32[4,128,64,128]{3,1,2,0:T(8,128)}), f32[4,128,64,128]{3,1,2,0:T(8,128)}, u32[]{:S(2)}, u32[]{:S(2)}) %all-to-all-start.5) | async-done | bytes 16777248 | tf_op jit(solution)/shard_map/all_to_all | solution.py:149
  1816.3 7.3 all-to-all-start.3
  1823.5 18.4 convolution_bitcast_fusion
  1842.0 163.3 %all-to-all-done.3 = f32[4,128,64,128]{3,1,2,0:T(8,128)} async-done(((f32[4,128,64,128]{3,1,2,0:T(8,128)}), f32[4,128,64,128]{3,1,2,0:T(8,128)}, u32[]{:S(2)}, u32[]{:S(2)}) %all-to-all-start.3) | async-done | bytes 16777248 | tf_op jit(solution)/shard_map/all_to_all | solution.py:149
  2005.3 17.4 convolution_bitcast_fusion.1
  2022.7 0.0 copy-done.2
  2022.8 11.4 pad_maximum_fusion
  (17 shorter events, 0.1 us)
Async XLA Ops:
  18.9 190.8 %all-to-all-start = ((f32[4,128,64,128]{1,3,2,0:T(8,128)}), f32[4,128,64,128]{1,3,2,0:T(8,128)}, u32[]{:S(2)}, u32[]{:S(2)}) async-start(f32[4,128,64,128]{1,3,2,0:T(8,128)} %fusion.84), calls=%async_computation | async-start | bytes 33554432 | tf_op jit(solution)/shard_map/all_to_all | solution.py:96
  227.2 23.7 %copy-start.9 = (f32[512,1024]{1,0:T(8,128)S(1)}, f32[512,1024]{1,0:T(8,128)}, u32[]{:S(2)}) copy-start(f32[512,1024]{1,0:T(8,128)} %constant.174.clone) | copy-start | bytes 6291460
  299.7 6.1 copy-start.5
  299.7 369.7 %all-to-all-start.1 = ((f32[8,64,64,128]{3,2,1,0:T(8,128)}), f32[8,64,64,128]{3,2,1,0:T(8,128)}, u32[]{:S(2)}, u32[]{:S(2)}) async-start(f32[8,64,64,128]{3,2,1,0:T(8,128)} %bitcast.100), calls=%async_computation.1 | async-start | bytes 33554432 | tf_op jit(solution)/shard_map/all_to_all | solution.py:100
  698.1 23.7 %copy-start.8 = (f32[512,1024]{1,0:T(8,128)S(1)}, f32[512,1024]{1,0:T(8,128)}, u32[]{:S(2)}) copy-start(f32[512,1024]{1,0:T(8,128)} %constant.176.clone) | copy-start | bytes 6291460
  752.2 6.2 copy-start.3
  837.1 7.3 copy-start.7
  887.9 369.3 %all-to-all-start.4 = ((f32[8,64,64,128]{3,1,2,0:T(8,128)}), f32[8,64,64,128]{3,1,2,0:T(8,128)}, u32[]{:S(2)}, u32[]{:S(2)}) async-start(f32[8,64,64,128]{3,1,2,0:T(8,128)} %copy.60), calls=%async_computation.4 | async-start | bytes 33554432 | tf_op jit(solution)/shard_map/all_to_all | solution.py:143
  1257.2 369.6 %all-to-all-start.2 = ((f32[8,64,64,128]{3,1,2,0:T(8,128)}), f32[8,64,64,128]{3,1,2,0:T(8,128)}, u32[]{:S(2)}, u32[]{:S(2)}) async-start(f32[8,64,64,128]{3,1,2,0:T(8,128)} %copy.55), calls=%async_computation.2 | async-start | bytes 33554432 | tf_op jit(solution)/shard_map/all_to_all | solution.py:143
  1274.2 16.4 copy-start.1
  1274.2 16.4 copy-start.6
  1626.8 189.4 %all-to-all-start.5 = ((f32[4,128,64,128]{3,1,2,0:T(8,128)}), f32[4,128,64,128]{3,1,2,0:T(8,128)}, u32[]{:S(2)}, u32[]{:S(2)}) async-start(f32[4,128,64,128]{3,1,2,0:T(8,128)} %copy.62), calls=%async_computation.5 | async-start | bytes 33554432 | tf_op jit(solution)/shard_map/all_to_all | solution.py:149
  1645.0 15.9 copy-start
  1709.0 114.5 %copy-start.4 = (f32[4,128,512,1]{2,1,3,0:T(8,128)S(1)}, f32[4,128,512,1]{2,1,3,0:T(8,128)}, u32[]{:S(2)}) copy-start(f32[4,128,512,1]{2,1,3,0:T(8,128)} %constant.181) | copy-start | bytes 3145732
  1816.3 189.0 %all-to-all-start.3 = ((f32[4,128,64,128]{3,1,2,0:T(8,128)}), f32[4,128,64,128]{3,1,2,0:T(8,128)}, u32[]{:S(2)}, u32[]{:S(2)}) async-start(f32[4,128,64,128]{3,1,2,0:T(8,128)} %copy.57), calls=%async_computation.3 | async-start | bytes 33554432 | tf_op jit(solution)/shard_map/all_to_all | solution.py:149
  2005.3 17.5 copy-start.2
